TPU v7x, 32 devices: a whole 2x2x4 slice. The times are simulated.
32 devices in a mesh: movie: 16 (over z, y, x), user: 2 (over core).
Axes of the slice: x: 2, y: 2, z: 4, core: 2. Of those that a mesh axis runs over, the one named last changes fastest.
Arguments:
- movie_ids: int32 [128, 128], P(('movie', 'user')), may hold values from 0 to 17919, as said below
- ratings: int32 [128, 128], P(('movie', 'user')), may hold values from 0 to 4
- valid: int32 [128, 128], P(('movie', 'user')), may hold values from 0 to 1, as said below
- weights: bfloat16 [5, 17920, 1024], P(None, 'movie'), may hold values from -0.5 to 0.5
- vis_bias: float32 [5, 17920], P(None, 'movie'), may hold values from -5 to 260
- hid_bias: float32 [1024], replicated, may hold values from -5 to 5
Outputs:
- weight_grad: float32 [5, 17920, 1024], P(None, 'movie')
- visible_grad: float32 [5, 17920], P(None, 'movie')
- hidden_grad: float32 [1024], replicated
- positive_hidden: float32 [128, 1024], P(('movie', 'user'))
Inputs may be any that keep to these rules, and one draw needn't show every extreme that they name: `movie_ids`: movie ids within one user's block are distinct. Of the slots with valid 1 among the users of one device (4 consecutive users), at most 96 name movies of any one block of 1120 consecutive movie ids; in every draw some such block takes exactly 96 from the users of every device. Slots with valid 0 are padding and count nowhere.
All inputs are finite; a program needn't handle non-finite values.
Results may differ from a plain program's by a relative error of at most 0.0054.
Values may be sent and summed in bfloat16 or wider, within the bound.
No kernel may reach another device: no remote copies, remote signals or barrier semaphores. Data moves between devices by JAX's collectives and lax.ppermute only.
A program may use at most 128 MiB of HBM per device.

v0:
```python
import jax
import jax.numpy as jnp
from jax import lax
from jax.sharding import PartitionSpec as P


def reconstruct(hidden_rows, weight_table, bias_row, rated_mask, levels):
    group_rows = hidden_rows.shape[0]
    rating_logits = (
        lax.dot_general(
            hidden_rows, weight_table, (((1,), (1,)), ((), ())), preferred_element_type=jnp.float32
        )
        + bias_row[None, :]
    )
    shaped = rating_logits.reshape(group_rows, levels, -1)
    largest = jnp.max(shaped, axis=1, keepdims=True)
    exponent = jnp.exp(shaped - largest)
    softened = (exponent / jnp.sum(exponent, axis=1, keepdims=True)).astype(jnp.bfloat16)
    return (softened * rated_mask[:, None, :]).reshape(group_rows, -1)


def hidden_phase(visible, weight_table, hid_bias, local_users, device_index):
    combined = jnp.dot(visible, weight_table, preferred_element_type=jnp.float32)
    all_probs = jax.nn.sigmoid(hid_bias[None, :] + lax.psum(combined, "movie"))
    own_rows = lax.dynamic_slice_in_dim(all_probs, device_index * local_users, local_users, 0)
    return (own_rows, all_probs.astype(jnp.bfloat16))


def on_device(movie_ids, ratings, valid, weights, vis_bias, hid_bias):
    owners = lax.axis_size("movie")
    device_index = lax.axis_index("movie")
    local_users, slot_count = movie_ids.shape
    levels, local_movies, hidden = weights.shape
    columns = levels * local_movies
    group_rows = owners * local_users
    capacity = max(2, 3 * local_users * slot_count // owners)
    flat_ids = movie_ids.reshape(-1)
    owner_ids = flat_ids // local_movies
    column_ids = ratings.reshape(-1) * local_movies + flat_ids % local_movies
    user_ids = jnp.arange(local_users * slot_count, dtype=jnp.int32) // slot_count
    usable = valid.reshape(-1) == 1
    matches = (owner_ids[:, None] == jnp.arange(owners, dtype=jnp.int32)[None, :]) & usable[:, None]
    ranking = jnp.cumsum(matches.astype(jnp.int32), axis=0) - 1
    placed = jnp.sum(jnp.where(matches, ranking, 0), axis=1)
    target = jnp.where(usable, owner_ids, owners)
    user_slots = (
        jnp.zeros((owners, capacity), jnp.int32).at[target, placed].set(user_ids, mode="drop")
    )
    column_slots = (
        jnp.full((owners, capacity), -1, jnp.int32).at[target, placed].set(column_ids, mode="drop")
    )
    got_users, got_columns = (
        lax.all_to_all(user_slots, "movie", split_axis=0, concat_axis=0, tiled=True),
        lax.all_to_all(column_slots, "movie", split_axis=0, concat_axis=0, tiled=True),
    )
    user_hot = (got_users[:, :, None] == jnp.arange(local_users, dtype=jnp.int32)).astype(
        jnp.bfloat16
    )
    column_hot = (got_columns[:, :, None] == jnp.arange(columns, dtype=jnp.int32)).astype(
        jnp.bfloat16
    )
    shown = jnp.einsum("ncu,ncj->nuj", user_hot, column_hot, preferred_element_type=jnp.float32)
    shown = shown.reshape(group_rows, columns).astype(jnp.bfloat16)
    rated_mask = jnp.sum(shown.reshape(group_rows, levels, local_movies), axis=1)
    weight_table = weights.reshape(columns, hidden)
    positive_own, positive_group = hidden_phase(
        shown, weight_table, hid_bias, local_users, device_index
    )
    reconstructed_ratings = reconstruct(
        positive_group, weight_table, vis_bias.reshape(columns), rated_mask, levels
    )
    negative_own, negative_group = hidden_phase(
        reconstructed_ratings, weight_table, hid_bias, local_users, device_index
    )
    contract = (((0,), (0,)), ((), ()))
    weight_grad = lax.dot_general(
        shown, positive_group, contract, preferred_element_type=jnp.float32
    )
    weight_grad = weight_grad - lax.dot_general(
        reconstructed_ratings, negative_group, contract, preferred_element_type=jnp.float32
    )
    visible_grad = jnp.sum(shown.astype(jnp.float32), axis=0) - jnp.sum(
        reconstructed_ratings.astype(jnp.float32), axis=0
    )
    weight_grad, visible_grad = lax.psum((weight_grad, visible_grad), "user")
    hidden_grad = lax.psum(jnp.sum(positive_own - negative_own, axis=0), ("movie", "user"))
    return (
        weight_grad.reshape(levels, local_movies, hidden),
        visible_grad.reshape(levels, local_movies),
        hidden_grad,
        positive_own,
    )


def solution(mesh):
    in_specs = (
        P(("movie", "user"), None),
        P(("movie", "user"), None),
        P(("movie", "user"), None),
        P(None, "movie", None),
        P(None, "movie"),
        P(),
    )
    out_specs = (P(None, "movie", None), P(None, "movie"), P(), P(("movie", "user"), None))
    return jax.shard_map(
        on_device, mesh=mesh, in_specs=in_specs, out_specs=out_specs, check_vma=False
    )
```

profile of v0, /device:TPU:0, one launch (start us, length us, event | category | flops | bytes accessed | tf_op | source)
XLA Modules:
  0.0 498.8 jit_solution(16229236096760497218)
XLA Ops:
  10.7 1.2 reduce-window.6
  12.8 70.4 %scatter_fusion.1 = s32[16,96]{1,0:T(8,128)} fusion(s32[16,96]{1,0:T(8,128)} %broadcast_in_dim.15, s32[512]{0:T(512)S(1)} %bitcast.81, s32[512]{0:T(512)S(1)} %get-tuple-element.10), kind=kCustom, calls=%fused_computation.1 | custom fusion | bytes 10240 | tf_op jit(solution)/shard_map/scatter | solution.py:50
  83.2 8.4 %all-to-all-start.1 = ((s32[16,1,96]{2,1,0:T(1,128)}), s32[16,1,96]{2,1,0:T(1,128)S(1)}, u32[]{:S(2)}, u32[]{:S(2)}) async-start(s32[16,1,96]{2,1,0:T(1,128)} %bitcast.13), calls=%async_computation.1 | async-start | bytes 16384 | tf_op jit(solution)/shard_map/all_to_all | solution.py:54
  91.7 25.2 %scatter_fusion = s32[16,96]{1,0:T(8,128)S(1)} fusion(s32[16,96]{1,0:T(8,128)S(1)} %broadcast_in_dim.12, s32[512]{0:T(512)S(1)} %bitcast.82, s32[512]{0:T(512)S(1)} %add_select_fusion.1), kind=kCustom, calls=%fused_computation | custom fusion | bytes 10240 | tf_op jit(solution)/shard_map/scatter | solution.py:47
  116.9 14.0 %all_to_all.18 = s32[16,1,96]{2,1,0:T(1,128)S(1)} all-to-all(s32[16,1,96]{2,1,0:T(1,128)S(1)} %bitcast.75), channel_id=1, replica_groups=mesh['movie'=16,'user'=2] {'movie'}, dimensions={0} | all-to-all | bytes 12288 | tf_op jit(solution)/shard_map/all_to_all | solution.py:53
  130.9 6.6 %convert_reduce_fusion.1 = (f32[5600]{0:T(1024)S(1)}, bf16[16,4,5600]{2,1,0:T(4,128)(2,1)S(1)}) fusion(s32[16,96]{1,0:T(8,128)S(1)} %bitcast.85, s32[16,96]{1,0:T(8,128)S(1)} %bitcast.86), kind=kOutput, calls=%fused_computation.12 | convolution fusion | flops 78490144 | bytes 751488 | tf_op jit(solution)/shard_map/ncu,ncj->nuj/dot_general | solution.py:62
  137.8 7.3 %fusion.24 = f32[64,1024]{1,0:T(8,128)} fusion(bf16[64,5600]{1,0:T(8,128)(2,1)S(1)} %convert_element_type.42, bf16[5600,1024]{1,0:T(8,128)(2,1)} %bitcast.77), kind=kOutput, calls=%fused_computation.65 | convolution fusion | flops 734003200 | bytes 12447744 | tf_op jit(solution)/shard_map/dot_general | solution.py:23
  147.2 1.1 mul.26
  148.3 2.7 mul.27
  151.1 98.4 %all-reduce.4.cloned.1.call-done = f32[64,1024]{1,0:T(8,128)} async-done(((f32[64,1024]{1,0:T(8,128)}), f32[64,1024]{1,0:T(8,128)}) %all-reduce.4.cloned.1.call-update) | async-done | bytes 262160 | tf_op jit(solution)/shard_map/psum | solution.py:24
  250.5 11.1 %fusion.9 = f32[5600,1024]{1,0:T(8,128)} fusion(bf16[64,5600]{1,0:T(8,128)(2,1)} %copy-done.1, f32[64,1024]{1,0:T(8,128)S(1)} %add_divide_fusion.1), kind=kOutput, calls=%fused_computation.22 | convolution fusion | flops 734068736 | bytes 23916544 | tf_op jit(solution)/shard_map/dot_general | solution.py:76
  261.7 4.7 convolution_add_fusion
  266.4 1.9 reshape.182
  270.8 7.1 %convolution_bitcast_fusion = f32[64,1024]{1,0:T(8,128)} fusion(bf16[5,1120,1024]{2,1,0:T(8,128)(2,1)} %param.9, bf16[64,5,1120]{2,1,0:T(8,128)(2,1)S(1)} %fusion.4), kind=kOutput, calls=%fused_computation.15 | convolution fusion | flops 734003200 | bytes 12447744 | tf_op jit(solution)/shard_map/dot_general | solution.py:23
  278.3 1.6 sub.52
  280.0 1.6 div.54
  281.5 3.0 div.55
  284.5 3.0 convert_reduce_fusion
  287.5 97.3 %all-reduce.6.cloned.1.call-done = f32[64,1024]{1,0:T(8,128)} async-done(((f32[64,1024]{1,0:T(8,128)}), f32[64,1024]{1,0:T(8,128)}) %all-reduce.6.cloned.1.call-update) | async-done | bytes 262160 | tf_op jit(solution)/shard_map/psum | solution.py:24
  385.8 15.5 %convolution_subtract_fusion = f32[5600,1024]{1,0:T(8,128)} fusion(f32[5600,1024]{1,0:T(8,128)} %fusion.9, bf16[64,5600]{1,0:T(8,128)(2,1)} %get-tuple-element.7, f32[64,1024]{1,0:T(8,128)S(1)} %add_divide_fusion), kind=kOutput, calls=%fused_computation.5 | convolution fusion | flops 739803136 | bytes 46854144 | tf_op jit(solution)/shard_map/dot_general | solution.py:79
  401.4 4.0 psum.38
  406.1 39.4 %psum.39 = f32[1024]{0:T(1024)} all-reduce(f32[1024]{0:T(1024)S(1)} %get-tuple-element.4), channel_id=1, replica_groups=mesh['movie'=16,'user'=2] {'movie','user'}, use_global_device_ids=true, to_apply=%region_15.16 | all-reduce | flops 1024 | bytes 8192 | tf_op jit(solution)/shard_map/psum | solution.py:86
  445.4 30.3 %all-reduce.8.cloned.1.call-done = f32[5,1120,1024]{2,1,0:T(8,128)} async-done(((f32[5,1120,1024]{2,1,0:T(8,128)}), f32[5,1120,1024]{2,1,0:T(8,128)}) %all-reduce.8.cloned.1.call-update) | async-done | bytes 22937616 | tf_op jit(solution)/shard_map/psum | solution.py:85
  475.8 16.5 %copy.37 = f32[5,1120,1024]{2,1,0:T(8,128)} copy(f32[5,1120,1024]{2,1,0:T(8,128)} %all-reduce.8.cloned.1.call-done) | data formatting | bytes 45875200
  (51 shorter events, 12.5 us)
Async XLA Ops:
  83.2 33.7 %all-to-all-start.1 = ((s32[16,1,96]{2,1,0:T(1,128)}), s32[16,1,96]{2,1,0:T(1,128)S(1)}, u32[]{:S(2)}, u32[]{:S(2)}) async-start(s32[16,1,96]{2,1,0:T(1,128)} %bitcast.13), calls=%async_computation.1 | async-start | bytes 16384 | tf_op jit(solution)/shard_map/all_to_all | solution.py:54
  91.6 157.9 %all-reduce.4.cloned.1.call-start = ((), (), s32[]{:S(2)}) async-start(), calls=%async_computation.2 | async-start | bytes 524288 | tf_op jit(solution)/shard_map/psum | solution.py:24
  137.8 7.4 %copy-start.1 = (bf16[64,5600]{1,0:T(8,128)(2,1)}, bf16[64,5600]{1,0:T(8,128)(2,1)S(1)}, u32[]{:S(2)}) copy-start(bf16[64,5600]{1,0:T(8,128)(2,1)S(1)} %convert_element_type.42) | copy-start | bytes 2150404
  137.8 7.6 %copy-start.3 = (f32[5,1120]{1,0:T(8,128)S(1)}, f32[5,1120]{1,0:T(8,128)}, u32[]{:S(2)}) copy-start(f32[5,1120]{1,0:T(8,128)} %param.10) | copy-start | bytes 67204
  145.2 239.6 %all-reduce.6.cloned.1.call-start = ((), (), s32[]{:S(2)}) async-start(), calls=%async_computation.3 | async-start | bytes 524288 | tf_op jit(solution)/shard_map/psum | solution.py:24
  146.4 103.1 %copy-start.4 = (f32[1024]{0:T(1024)S(1)}, f32[1024]{0:T(1024)}, u32[]{:S(2)}) copy-start(f32[1024]{0:T(1024)} %param.11) | copy-start | bytes 12292
  148.3 113.3 %slice-start = ((s8[11468800]{0:T(1024)(128)(4,1)}), s8[3080192]{0:T(1024)(128)(4,1)S(1)}, s32[]{:S(2)}) async-start(s8[11468800]{0:T(1024)(128)(4,1)} %bitcast.78), calls=%async_computation.5 | async-start | bytes 6160384
  250.5 11.2 %slice-start.1 = ((s8[11468800]{0:T(1024)(128)(4,1)}), s8[4194304]{0:T(1024)(128)(4,1)S(1)}, s32[]{:S(2)}) async-start(s8[11468800]{0:T(1024)(128)(4,1)} %bitcast.78), calls=%async_computation.6 | async-start | bytes 8388608
  250.5 11.2 %slice-start.2 = ((s8[11468800]{0:T(1024)(128)(4,1)}), s8[4194304]{0:T(1024)(128)(4,1)S(1)}, s32[]{:S(2)}) async-start(s8[11468800]{0:T(1024)(128)(4,1)} %bitcast.78), calls=%async_computation.7 | async-start | bytes 8388608
  277.9 197.9 %all-reduce.8.cloned.1.call-start = ((), (), s32[]{:S(2)}) async-start(), calls=%async_computation.4 | async-start | bytes 45875200 | tf_op jit(solution)/shard_map/psum | solution.py:85
  281.5 3.0 copy-start
  281.5 3.0 copy-start.2
Sparse Core Ops, SparseCore 0:
  145.3 104.1 all-reduce.3
  278.0 106.6 all-reduce.5
  401.4 74.2 all-reduce.7
where the time goes:
time: 501 us; the launch traced here: 499 us
  waiting for transfers between devices  226 us (45%)
  local copies, waits for them, and re-layouts  126 us (25%)
  blocking collectives  57.4 us (11%)
  matrix products  52.3 us (10%)
  between operations  14 us (3%)
  other arithmetic  13.7 us (3%)
  starting transfers between devices  8.93 us (2%)
    psum x2, waiting for transfers between devices, hidden_phase(): all_probs = jax.nn.sigmoid(hid_bias[None, :] + lax.psum(combined, 'movie'))  196 us
    scatter x1, local copies, waits for them, and re-layouts, on_device(): jnp.full((owners, capacity), -1, jnp.int32).at[target, placed]  70.4 us
    psum x1, blocking collectives, on_device(): lax.psum(jnp.sum(positive_own - negative_own, axis=0), ('movie', 'user'))  39.4 us
    psum x1, waiting for transfers between devices, on_device(): weight_grad, visible_grad = lax.psum((weight_grad, visible_grad), 'user')  30.3 us
    scatter x1, local copies, waits for them, and re-layouts, on_device(): jnp.zeros((owners, capacity), jnp.int32).at[target, placed]  25.2 us
    unnamed x17, local copies, waits for them, and re-layouts  16.6 us
    dot_general x1, matrix products, on_device(): lax.dot_general(reconstructed_ratings, negative_group, contract, preferre...  15.5 us
    dot_general x2, matrix products, hidden_phase(): jnp.dot(visible, weight_table, preferred_element_type=jnp.float32)  14.4 us
  transfers between devices with their start and end apart: 4, of which 3 were waited for; matrix products, arithmetic and copies ran while one was open for 8% of the time, Pallas kernels for 0%

commit v1 on v0

--- a/solution.py
+++ b/solution.py
@@ -83,7 +83,9 @@
         reconstructed_ratings.astype(jnp.float32), axis=0
     )
     weight_grad, visible_grad = lax.psum((weight_grad, visible_grad), "user")
-    hidden_grad = lax.psum(jnp.sum(positive_own - negative_own, axis=0), ("movie", "user"))
+    hidden_grad = jnp.sum(
+        lax.all_gather(jnp.sum(positive_own - negative_own, axis=0), ("movie", "user")), axis=0
+    )
     return (
         weight_grad.reshape(levels, local_movies, hidden),
         visible_grad.reshape(levels, local_movies),

time: 501 us -> 501 us (level)
    all_gather x0 -> x1, blocking collectives: none -> 39.9 us  [on_device(): lax.all_gather(jnp.sum(positive_own - negative_own, axis=0), ('movie', 'u...]
    psum x1 -> x0, blocking collectives: 39.4 us -> none  [on_device(): lax.psum(jnp.sum(positive_own - negative_own, axis=0), ('movie', 'user'))]
where the time goes in v1:
time: 501 us; the launch traced here: 499 us
  waiting for transfers between devices  225 us (45%)
  local copies, waits for them, and re-layouts  126 us (25%)
  blocking collectives  57.9 us (12%)
  matrix products  52.3 us (10%)
  other arithmetic  14.3 us (3%)
  between operations  14 us (3%)
  starting transfers between devices  8.93 us (2%)
    psum x2, waiting for transfers between devices, hidden_phase(): all_probs = jax.nn.sigmoid(hid_bias[None, :] + lax.psum(combined, 'movie'))  196 us
    scatter x1, local copies, waits for them, and re-layouts, on_device(): jnp.full((owners, capacity), -1, jnp.int32).at[target, placed]  70.4 us
    all_gather x1, blocking collectives, on_device(): lax.all_gather(jnp.sum(positive_own - negative_own, axis=0), ('movie', 'u...  39.9 us
    psum x1, waiting for transfers between devices, on_device(): weight_grad, visible_grad = lax.psum((weight_grad, visible_grad), 'user')  29.2 us
    scatter x1, local copies, waits for them, and re-layouts, on_device(): jnp.zeros((owners, capacity), jnp.int32).at[target, placed]  25.2 us
    unnamed x17, local copies, waits for them, and re-layouts  16.6 us
    dot_general x1, matrix products, on_device(): lax.dot_general(reconstructed_ratings, negative_group, contract, preferre...  15.5 us
    dot_general x2, matrix products, hidden_phase(): jnp.dot(visible, weight_table, preferred_element_type=jnp.float32)  14.4 us
  transfers between devices with their start and end apart: 4, of which 3 were waited for; matrix products, arithmetic and copies ran while one was open for 8% of the time, Pallas kernels for 0%

profile of v1, /device:TPU:0, one launch (start us, length us, event | category | flops | bytes accessed | tf_op | source)
XLA Modules:
  0.0 498.8 jit_solution(16024511404043122188)
XLA Ops:
  10.7 1.2 reduce-window.6
  12.8 70.4 %scatter_fusion.1 = s32[16,96]{1,0:T(8,128)} fusion(s32[16,96]{1,0:T(8,128)} %broadcast_in_dim.15, s32[512]{0:T(512)S(1)} %bitcast.81, s32[512]{0:T(512)S(1)} %get-tuple-element.10), kind=kCustom, calls=%fused_computation.1 | custom fusion | bytes 10240 | tf_op jit(solution)/shard_map/scatter | solution.py:50
  83.2 8.4 %all-to-all-start.1 = ((s32[16,1,96]{2,1,0:T(1,128)}), s32[16,1,96]{2,1,0:T(1,128)S(1)}, u32[]{:S(2)}, u32[]{:S(2)}) async-start(s32[16,1,96]{2,1,0:T(1,128)} %bitcast.13), calls=%async_computation.1 | async-start | bytes 16384 | tf_op jit(solution)/shard_map/all_to_all | solution.py:54
  91.7 25.2 %scatter_fusion = s32[16,96]{1,0:T(8,128)S(1)} fusion(s32[16,96]{1,0:T(8,128)S(1)} %broadcast_in_dim.12, s32[512]{0:T(512)S(1)} %bitcast.82, s32[512]{0:T(512)S(1)} %add_select_fusion.1), kind=kCustom, calls=%fused_computation | custom fusion | bytes 10240 | tf_op jit(solution)/shard_map/scatter | solution.py:47
  116.9 14.0 %all_to_all.18 = s32[16,1,96]{2,1,0:T(1,128)S(1)} all-to-all(s32[16,1,96]{2,1,0:T(1,128)S(1)} %bitcast.75), channel_id=1, replica_groups=mesh['movie'=16,'user'=2] {'movie'}, dimensions={0} | all-to-all | bytes 12288 | tf_op jit(solution)/shard_map/all_to_all | solution.py:53
  130.9 6.6 %convert_reduce_fusion.1 = (f32[5600]{0:T(1024)S(1)}, bf16[16,4,5600]{2,1,0:T(4,128)(2,1)S(1)}) fusion(s32[16,96]{1,0:T(8,128)S(1)} %bitcast.85, s32[16,96]{1,0:T(8,128)S(1)} %bitcast.86), kind=kOutput, calls=%fused_computation.12 | convolution fusion | flops 78490144 | bytes 751488 | tf_op jit(solution)/shard_map/ncu,ncj->nuj/dot_general | solution.py:62
  137.8 7.3 %fusion.24 = f32[64,1024]{1,0:T(8,128)} fusion(bf16[64,5600]{1,0:T(8,128)(2,1)S(1)} %convert_element_type.42, bf16[5600,1024]{1,0:T(8,128)(2,1)} %bitcast.77), kind=kOutput, calls=%fused_computation.65 | convolution fusion | flops 734003200 | bytes 12447744 | tf_op jit(solution)/shard_map/dot_general | solution.py:23
  147.2 1.1 mul.26
  148.3 2.7 mul.27
  151.1 98.4 %all-reduce.4.cloned.1.call-done = f32[64,1024]{1,0:T(8,128)} async-done(((f32[64,1024]{1,0:T(8,128)}), f32[64,1024]{1,0:T(8,128)}) %all-reduce.4.cloned.1.call-update) | async-done | bytes 262160 | tf_op jit(solution)/shard_map/psum | solution.py:24
  250.5 11.1 %fusion.9 = f32[5600,1024]{1,0:T(8,128)} fusion(bf16[64,5600]{1,0:T(8,128)(2,1)} %copy-done.1, f32[64,1024]{1,0:T(8,128)S(1)} %add_divide_fusion.1), kind=kOutput, calls=%fused_computation.22 | convolution fusion | flops 734068736 | bytes 23916544 | tf_op jit(solution)/shard_map/dot_general | solution.py:76
  261.7 4.7 convolution_add_fusion
  266.4 1.9 reshape.182
  270.8 7.1 %convolution_bitcast_fusion = f32[64,1024]{1,0:T(8,128)} fusion(bf16[5,1120,1024]{2,1,0:T(8,128)(2,1)} %param.9, bf16[64,5,1120]{2,1,0:T(8,128)(2,1)S(1)} %fusion.4), kind=kOutput, calls=%fused_computation.15 | convolution fusion | flops 734003200 | bytes 12447744 | tf_op jit(solution)/shard_map/dot_general | solution.py:23
  278.3 1.6 sub.52
  280.0 1.6 div.54
  281.5 3.0 div.55
  284.5 3.0 convert_reduce_fusion
  287.5 97.3 %all-reduce.6.cloned.1.call-done = f32[64,1024]{1,0:T(8,128)} async-done(((f32[64,1024]{1,0:T(8,128)}), f32[64,1024]{1,0:T(8,128)}) %all-reduce.6.cloned.1.call-update) | async-done | bytes 262160 | tf_op jit(solution)/shard_map/psum | solution.py:24
  385.8 15.5 %convolution_subtract_fusion = f32[5600,1024]{1,0:T(8,128)} fusion(f32[5600,1024]{1,0:T(8,128)} %fusion.9, bf16[64,5600]{1,0:T(8,128)(2,1)} %get-tuple-element.7, f32[64,1024]{1,0:T(8,128)S(1)} %add_divide_fusion), kind=kOutput, calls=%fused_computation.5 | convolution fusion | flops 739803136 | bytes 46854144 | tf_op jit(solution)/shard_map/dot_general | solution.py:79
  401.4 4.0 psum.31
  406.0 39.9 %all-gather = f32[32768]{0:T(1024)S(1)} all-gather(f32[1024]{0:T(1024)S(1)} %get-tuple-element.4), channel_id=2, replica_groups=mesh['movie'=16,'user'=2] {'movie','user'}, dimensions={0}, use_global_device_ids=true | all-gather | bytes 135168 | tf_op jit(solution)/shard_map/all_gather | solution.py:87
  446.5 29.2 %all-reduce.8.cloned.1.call-done = f32[5,1120,1024]{2,1,0:T(8,128)} async-done(((f32[5,1120,1024]{2,1,0:T(8,128)}), f32[5,1120,1024]{2,1,0:T(8,128)}) %all-reduce.8.cloned.1.call-update) | async-done | bytes 22937616 | tf_op jit(solution)/shard_map/psum | solution.py:85
  475.8 16.5 %copy.41 = f32[5,1120,1024]{2,1,0:T(8,128)} copy(f32[5,1120,1024]{2,1,0:T(8,128)} %all-reduce.8.cloned.1.call-done) | data formatting | bytes 45875200
  (53 shorter events, 13.2 us)
Async XLA Ops:
  83.2 33.7 %all-to-all-start.1 = ((s32[16,1,96]{2,1,0:T(1,128)}), s32[16,1,96]{2,1,0:T(1,128)S(1)}, u32[]{:S(2)}, u32[]{:S(2)}) async-start(s32[16,1,96]{2,1,0:T(1,128)} %bitcast.13), calls=%async_computation.1 | async-start | bytes 16384 | tf_op jit(solution)/shard_map/all_to_all | solution.py:54
  91.6 157.9 %all-reduce.4.cloned.1.call-start = ((), (), s32[]{:S(2)}) async-start(), calls=%async_computation.2 | async-start | bytes 524288 | tf_op jit(solution)/shard_map/psum | solution.py:24
  137.8 7.4 %copy-start.1 = (bf16[64,5600]{1,0:T(8,128)(2,1)}, bf16[64,5600]{1,0:T(8,128)(2,1)S(1)}, u32[]{:S(2)}) copy-start(bf16[64,5600]{1,0:T(8,128)(2,1)S(1)} %convert_element_type.42) | copy-start | bytes 2150404
  137.8 7.6 %copy-start.3 = (f32[5,1120]{1,0:T(8,128)S(1)}, f32[5,1120]{1,0:T(8,128)}, u32[]{:S(2)}) copy-start(f32[5,1120]{1,0:T(8,128)} %param.10) | copy-start | bytes 67204
  145.2 239.6 %all-reduce.6.cloned.1.call-start = ((), (), s32[]{:S(2)}) async-start(), calls=%async_computation.3 | async-start | bytes 524288 | tf_op jit(solution)/shard_map/psum | solution.py:24
  146.4 103.1 %copy-start.4 = (f32[1024]{0:T(1024)S(1)}, f32[1024]{0:T(1024)}, u32[]{:S(2)}) copy-start(f32[1024]{0:T(1024)} %param.11) | copy-start | bytes 12292
  148.3 113.3 %slice-start = ((s8[11468800]{0:T(1024)(128)(4,1)}), s8[3080192]{0:T(1024)(128)(4,1)S(1)}, s32[]{:S(2)}) async-start(s8[11468800]{0:T(1024)(128)(4,1)} %bitcast.78), calls=%async_computation.5 | async-start | bytes 6160384
  250.5 11.2 %slice-start.1 = ((s8[11468800]{0:T(1024)(128)(4,1)}), s8[4194304]{0:T(1024)(128)(4,1)S(1)}, s32[]{:S(2)}) async-start(s8[11468800]{0:T(1024)(128)(4,1)} %bitcast.78), calls=%async_computation.6 | async-start | bytes 8388608
  250.5 11.2 %slice-start.2 = ((s8[11468800]{0:T(1024)(128)(4,1)}), s8[4194304]{0:T(1024)(128)(4,1)S(1)}, s32[]{:S(2)}) async-start(s8[11468800]{0:T(1024)(128)(4,1)} %bitcast.78), calls=%async_computation.7 | async-start | bytes 8388608
  277.9 197.9 %all-reduce.8.cloned.1.call-start = ((), (), s32[]{:S(2)}) async-start(), calls=%async_computation.4 | async-start | bytes 45875200 | tf_op jit(solution)/shard_map/psum | solution.py:85
  281.5 3.0 copy-start
  281.5 3.0 copy-start.2
Sparse Core Ops, SparseCore 0:
  145.3 104.1 all-reduce.3
  278.0 106.6 all-reduce.5
  401.4 74.3 all-reduce.7
